TPU v7x, 32 devices: a whole 2x2x4 slice. The times are simulated.
32 devices in a mesh: gx: 8 (over y, x, core), gy: 4 (over z).
Axes of the slice: x: 2, y: 2, z: 4, core: 2. Of those that a mesh axis runs over, the one named last changes fastest.
Arguments:
- queries: bfloat16 [512, 2048], P(('gx', 'gy')), may hold values from -6 to 6
- probe_dev: int32 [512, 16], P(('gx', 'gy')), may hold values from 0 to 31, all different within a row; in each aligned block of 16 rows (0 to 15, 16 to 31, ...) at most 10 rows name the same one
- probe_list: int32 [512, 16], P(('gx', 'gy')), may hold values from 0 to 15
- documents: bfloat16 [512, 256, 2048], P(('gx', 'gy')), may hold values from -6 to 6
- lengths: int32 [512], P(('gx', 'gy')), may hold values from 96 to 256, as said below
- short_dev: int32 [512, 32], P(('gx', 'gy')), may hold values from 0 to 31, all different within a row; in each aligned block of 16 rows (0 to 15, 16 to 31, ...) at most 16 rows name the same one
- short_list: int32 [512, 32], P(('gx', 'gy')), may hold values from 0 to 15
- short_row: int32 [512, 32], P(('gx', 'gy')), may hold values from 0 to 95
Outputs:
- prefix_top: float32 [512, 32], P(('gx', 'gy'))
- rescored: float32 [512, 32], P(('gx', 'gy'))
Inputs may be any that keep to these rules, and one draw needn't show every extreme that they name: `lengths`: every list holds at least 96 documents, and in every draw some list is full. `probe_dev`: the 16 entries of a query name different devices. Among the 16 queries of one device, no device is named more than 10 times, and some device is named exactly 10 times. `short_dev`: the 32 entries of a query name different devices. Among the 16 queries of one device, no device is named more than 16 times, and some device is named exactly 16 times.
All inputs are finite; a program needn't handle non-finite values.
Results may differ from a plain program's by a relative error of at most 0.0029.
Values may be sent and summed in bfloat16 or wider, within the bound.
A program may use at most 128 MiB of HBM per device.

v0:
```python
import functools

import jax
import jax.numpy as jnp
from jax import lax
from jax.experimental import pallas as pl
from jax.experimental.pallas import tpu as pltpu
from jax.sharding import PartitionSpec as P

PREFIX = 256
TOPK = 32
SHORT_ROWS = 96
AXES = ("gx", "gy")
LANES = 128
HALF = 64
NT = (((1,), (1,)), ((), ()))
MESH = pl.DeviceIdType.MESH


def unit_rows(values):
    return values / jnp.sqrt(1.0 + jnp.sum(values * values, axis=1, keepdims=True))


def sort_pairs(n):
    p = 1
    while p < n:
        k = p
        while k >= 1:
            for j in range(k % p, n - k, 2 * k):
                for i in range(min(k, n - j - k)):
                    if (i + j) // (2 * p) == (i + j + k) // (2 * p):
                        yield i + j, i + j + k
            k //= 2
        p *= 2


def sort_desc(v):
    v = list(v)
    for a, b in sort_pairs(len(v)):
        v[a], v[b] = jnp.maximum(v[a], v[b]), jnp.minimum(v[a], v[b])
    return v


def merge_top(a, b):
    n = len(a)
    v = [jnp.maximum(a[i], b[n - 1 - i]) for i in range(n)]
    step = n // 2
    while step:
        for i in range(n):
            if not i & step:
                v[i], v[i + step] = jnp.maximum(v[i], v[i + step]), jnp.minimum(v[i], v[i + step])
        step //= 2
    return v


def device_of(position):
    size = lax.axis_size("gy")
    return position // size, position % size


def gather_kernel(split, q_ref, code_ref, a_ref, b_ref, line_send, line_recv, cube_send, cube_recv):
    gx, gy = lax.axis_index("gx"), lax.axis_index("gy")
    line = lax.axis_size("gy")
    bits = len(a_ref.shape) - 3
    outs = (a_ref, b_ref)

    def flip(bit):
        size = 1 << bit
        return gx + (1 - 2 * ((gx // size) % 2)) * size

    def view(ref, free, slot):
        spots = [slice(None) if b in free else (gx // (1 << b)) % 2 for b in range(bits - 1, -1, -1)]
        return ref.at[tuple(spots) + (slot,)]

    barrier = pltpu.get_barrier_semaphore()
    for k in range(1, line):
        pl.semaphore_signal(barrier, inc=1, device_id=(gx, (gy + k) % line), device_id_type=MESH)
    for b in range(bits):
        pl.semaphore_signal(barrier, inc=1, device_id=(flip(b), gy), device_id_type=MESH)
    values = q_ref[...].astype(jnp.float32)
    unit = unit_rows(values).astype(jnp.bfloat16)
    view(a_ref, (), gy)[...] = unit[:, :split]
    rest = unit.shape[1] - split
    own = view(b_ref, (), gy)
    own[:, :rest] = unit[:, split:]
    own[:, rest:rest + PREFIX] = unit_rows(values[:, :PREFIX]).astype(jnp.bfloat16)
    own[:, rest + PREFIX:] = code_ref[...]
    pl.semaphore_wait(barrier, line - 1 + bits)

    offsets = sorted(range(1, line), key=lambda k: (min(k, line - k), k))

    def line_copy(piece, k):
        ref = outs[piece]
        return pltpu.make_async_remote_copy(
            src_ref=view(ref, (), gy), dst_ref=view(ref, (), gy),
            send_sem=line_send.at[piece, k], recv_sem=line_recv.at[piece, k],
            device_id=(gx, (gy + k) % line), device_id_type=MESH,
        )

    order = (list(range(1, bits)) + [0], list(range(bits - 1, 0, -1)) + [0])

    def cube_copy(piece, k, step):
        ref, slot = outs[piece], (gy + line - k) % line
        src = view(ref, order[piece][:step], slot)
        return pltpu.make_async_remote_copy(
            src_ref=src, dst_ref=src,
            send_sem=cube_send.at[piece, k, step], recv_sem=cube_recv.at[piece, k, step],
            device_id=(flip(order[piece][step]), gy), device_id_type=MESH,
        )

    steps = bits
    slots = [0] + offsets
    for k in offsets:
        for piece in range(2):
            line_copy(piece, k).start()
    for wave in range(len(slots) + steps):
        for step in range(steps, -1, -1):
            if not 0 <= wave - step < len(slots):
                continue
            k = slots[wave - step]
            for piece in range(2):
                if step == 0 and k:
                    line_copy(piece, k).wait_recv()
                if step > 0:
                    cube_copy(piece, k, step - 1).wait_recv()
                if step < steps:
                    cube_copy(piece, k, step).start()
    for piece in range(2):
        for k in offsets:
            line_copy(piece, k).wait_send()
        for k in slots:
            for step in range(steps):
                cube_copy(piece, k, step).wait_send()


def exchange_kernel(src_ref, out_ref, send_sem, recv_sem, own_sem):
    count = src_ref.shape[0]
    me = lax.axis_index("gx") * lax.axis_size("gy") + lax.axis_index("gy")
    barrier = pltpu.get_barrier_semaphore()

    @pl.loop(1, count)
    def _(k):
        pl.semaphore_signal(barrier, inc=1, device_id=device_of((me + k) % count), device_id_type=MESH)

    own = pltpu.make_async_copy(src_ref.at[me], out_ref.at[me], own_sem)
    own.start()
    pl.semaphore_wait(barrier, count - 1)

    def copy(k):
        peer = (me + k) % count
        return pltpu.make_async_remote_copy(
            src_ref=src_ref.at[peer], dst_ref=out_ref.at[me],
            send_sem=send_sem.at[k], recv_sem=recv_sem.at[k],
            device_id=device_of(peer), device_id_type=MESH,
        )

    @pl.loop(1, count)
    def _(k):
        copy(k).start()

    own.wait()

    @pl.loop(1, count)
    def _(k):
        copy(k).wait_recv()

    @pl.loop(1, count)
    def _(k):
        copy(k).wait_send()


def score_kernel(probes, shorts, a_ref, b_ref, len_ref, docs_ref, out_ref, pre_docs, top_docs, chosen, result, sems):
    lists, rows, full = docs_ref.shape
    total, split = a_ref.shape
    rest = full - split
    per_dev = 16
    me = (lax.axis_index("gx") * lax.axis_size("gy") + lax.axis_index("gy")).astype(jnp.float32)
    pre_copy = pltpu.make_async_copy(docs_ref.at[:, :, pl.ds(0, PREFIX)], pre_docs, sems.at[0])
    top_copy = pltpu.make_async_copy(docs_ref.at[:, pl.ds(0, SHORT_ROWS), :], top_docs, sems.at[1])
    pre_copy.start()
    top_copy.start()
    pre_copy.wait()
    top_copy.wait()
    tile = chosen.shape[1]
    chunk = 32
    group = 4
    result[...] = jnp.zeros_like(result)

    @pl.loop(0, total // tile)
    def _(block):
        mine = pl.ds(pl.multiple_of(block * tile, tile), tile)
        codes = jnp.transpose(b_ref[mine, rest + PREFIX:].astype(jnp.float32))
        p_dev, p_list = codes[:probes], codes[probes:2 * probes]
        base = 2 * probes
        s_dev, s_list, s_row = (codes[base + i * shorts:base + (i + 1) * shorts] for i in range(3))
        probed = jnp.sum(jnp.where(p_dev == me, p_list + 1.0, 0.0), axis=0, keepdims=True).astype(jnp.int32) - 1
        wanted = jnp.sum(jnp.where(s_dev == me, s_list * rows + s_row + 1.0, 0.0), axis=0, keepdims=True).astype(jnp.int32) - 1

        @pl.loop(0, rows // chunk)
        def _(c):
            first = pl.multiple_of(c * chunk, chunk)
            docs = pre_docs[:, pl.ds(first, chunk), :].reshape(lists * chunk, PREFIX)
            scores = lax.dot_general(docs, b_ref[mine, rest:rest + PREFIX], NT, preferred_element_type=jnp.float32)
            slot = lax.broadcasted_iota(jnp.int32, (chunk, tile), 0) + first
            value = jnp.full((chunk, tile), -jnp.inf, jnp.float32)
            for l in range(lists):
                limit = jnp.where(probed == l, len_ref[l], 0)
                value = jnp.where(slot < limit, scores[l * chunk:(l + 1) * chunk], value)
            chosen[pl.ds(first, chunk), :] = value

        @pl.loop(0, tile // LANES)
        def _(t):
            lanes = pl.ds(pl.multiple_of(t * LANES, LANES), LANES)
            v = [chosen[pl.ds(8 * i, 8), lanes] for i in range(rows // 8)]
            parts = [sort_desc(v[i:i + TOPK]) for i in range(0, len(v), TOPK)]
            v = functools.reduce(merge_top, parts)
            for shift in (4, 2, 1):
                v = merge_top(v, [pltpu.roll(x, shift, 0) for x in v])
            sub = lax.broadcasted_iota(jnp.int32, (8, LANES), 0)
            for a in range(TOPK // 8):
                packed = v[8 * a]
                for s in range(1, 8):
                    packed = jnp.where(sub == s, v[8 * a + s], packed)
                result[pl.ds(8 * a, 8), lanes] = packed

        def rescore(g, acc):
            docs = top_docs[pl.ds(g * group, group)].reshape(group * SHORT_ROWS, full)
            scores = lax.dot_general(docs[:, :split], a_ref[mine, :], NT, preferred_element_type=jnp.float32)
            scores = scores + lax.dot_general(docs[:, split:], b_ref[mine, :rest], NT, preferred_element_type=jnp.float32)
            slot = lax.broadcasted_iota(jnp.int32, (SHORT_ROWS, tile), 0)
            for j in range(group):
                hit = slot == wanted - (g * group + j) * rows
                part = jnp.where(hit, scores[j * SHORT_ROWS:(j + 1) * SHORT_ROWS], 0.0)
                acc = acc + jnp.sum(part.reshape(SHORT_ROWS // 8, 8, tile), axis=0)
            return acc

        acc = lax.fori_loop(0, lists // group, rescore, jnp.zeros((8, tile), jnp.float32))
        result[TOPK:TOPK + 8, :] = jnp.broadcast_to(jnp.sum(acc, axis=0, keepdims=True), (8, tile))
        lane = lax.broadcasted_iota(jnp.int32, (8, LANES), 1)
        for t in range(tile // LANES):
            turned = jnp.transpose(result[:, t * LANES:(t + 1) * LANES])
            for d in range(LANES // per_dev):
                low = turned[d * per_dev:d * per_dev + 8]
                high = pltpu.roll(turned[d * per_dev + 8:(d + 1) * per_dev], HALF, 1)
                out_ref[block * (tile // per_dev) + t * (LANES // per_dev) + d] = jnp.where(lane < HALF, low, high)


def merge_kernel(got_ref, dev_ref, top_ref, short_ref):
    count = got_ref.shape[0]
    shorts = dev_ref.shape[1]
    v = [got_ref[i] for i in range(count)]
    pad = -count % TOPK
    v = v + [jnp.full_like(v[0], -jnp.inf)] * pad
    parts = [sort_desc(v[i:i + TOPK]) for i in range(0, len(v), TOPK)]
    best = functools.reduce(merge_top, parts)
    shift = TOPK // 2
    while shift:
        best = merge_top(best, [pltpu.roll(x, LANES - shift, 1) for x in best])
        shift //= 2
    lane = lax.broadcasted_iota(jnp.int32, (8, LANES), 1)
    out = best[0]
    for i in range(1, TOPK):
        out = jnp.where(lane % HALF == i, pltpu.roll(best[i], i, 1), out)
    top_ref[0:8, :] = out[:, :TOPK]
    top_ref[8:16, :] = pltpu.roll(out, HALF, 1)[:, :TOPK]
    for h in range(2):
        dev = dev_ref[8 * h:8 * h + 8, :]
        acc = jnp.zeros((8, shorts), jnp.float32)
        for i in range(count):
            spot = HALF * h + TOPK
            acc = jnp.where(dev == i, jnp.broadcast_to(got_ref[i][:, spot:spot + 1], (8, shorts)), acc)
        short_ref[8 * h:8 * h + 8, :] = acc


def shards(queries, probe_dev, probe_list, documents, lengths, short_dev, short_list, short_row):
    count = lax.axis_size(AXES)
    lists, rows, full = documents.shape
    query_rows = queries.shape[0]
    probes, shorts = probe_dev.shape[1], short_dev.shape[1]
    codes = jnp.concatenate([probe_dev, probe_list, short_dev, short_list, short_row], axis=1)
    line = lax.axis_size("gy")
    bits = (count // line).bit_length() - 1
    split = (full + PREFIX + LANES + 2 * LANES - 1) // (2 * LANES) * LANES
    widths = (split, full - split + PREFIX + codes.shape[1])
    vmem = pl.BlockSpec(memory_space=pltpu.VMEM)
    everyone = pl.pallas_call(
        functools.partial(gather_kernel, split),
        out_shape=tuple(
            jax.ShapeDtypeStruct((2,) * bits + (line, query_rows, width), jnp.bfloat16) for width in widths
        ),
        in_specs=[vmem, vmem],
        out_specs=(vmem, vmem),
        scratch_shapes=[
            pltpu.SemaphoreType.DMA((2, line)),
            pltpu.SemaphoreType.DMA((2, line)),
            pltpu.SemaphoreType.DMA((2, line, bits)),
            pltpu.SemaphoreType.DMA((2, line, bits)),
        ],
        compiler_params=pltpu.CompilerParams(collective_id=0, has_side_effects=True),
        name="gather",
    )(queries, codes.astype(jnp.bfloat16))
    everyone = [x.reshape(-1, x.shape[-1]) for x in everyone]
    total = count * query_rows
    tile = min(512, total)
    returned = pl.pallas_call(
        functools.partial(score_kernel, probes, shorts),
        out_shape=jax.ShapeDtypeStruct((count, 8, LANES), jnp.float32),
        in_specs=[vmem, vmem, pl.BlockSpec(memory_space=pltpu.SMEM), pl.BlockSpec(memory_space=pl.ANY)],
        out_specs=vmem,
        scratch_shapes=[
            pltpu.VMEM((lists, rows, PREFIX), jnp.bfloat16),
            pltpu.VMEM((lists, SHORT_ROWS, full), jnp.bfloat16),
            pltpu.VMEM((rows, tile), jnp.float32),
            pltpu.VMEM((LANES, tile), jnp.float32),
            pltpu.SemaphoreType.DMA((2,)),
        ],
        compiler_params=pltpu.CompilerParams(vmem_limit_bytes=60 * 1024 * 1024),
        name="score",
    )(*everyone, lengths, documents)
    got = pl.pallas_call(
        exchange_kernel,
        out_shape=jax.ShapeDtypeStruct(returned.shape, returned.dtype),
        in_specs=[vmem],
        out_specs=vmem,
        scratch_shapes=[
            pltpu.SemaphoreType.DMA((count,)),
            pltpu.SemaphoreType.DMA((count,)),
            pltpu.SemaphoreType.DMA,
        ],
        compiler_params=pltpu.CompilerParams(collective_id=1, has_side_effects=True),
        name="exchange",
    )(returned)
    return pl.pallas_call(
        merge_kernel,
        out_shape=(
            jax.ShapeDtypeStruct((query_rows, TOPK), jnp.float32),
            jax.ShapeDtypeStruct((query_rows, shorts), jnp.float32),
        ),
        in_specs=[vmem, vmem],
        out_specs=(vmem, vmem),
        name="merge",
    )(got, short_dev)


def solution(mesh):
    one = P(AXES, None)
    in_specs = (one, one, one, P(AXES, None, None), P(AXES), one, one, one)
    return jax.shard_map(shards, mesh=mesh, in_specs=in_specs, out_specs=(one, one), check_vma=False)
```

profile of v0, /device:TPU:0, one launch (start us, length us, event | category | flops | bytes accessed | tf_op | source)
XLA Modules:
  0.0 61.7 jit_solution(1122394069509481892)
XLA Ops:
  0.6 0.7 %convert.15 = bf16[16,16]{1,0:T(8,128)(2,1)S(1)} convert(s32[16,16]{1,0:T(8,128)} %param.9) | non-fusion elementwise | flops 256 | bytes 1536 | tf_op jit(solution)/shard_map/convert
  1.3 0.7 %convert.16 = bf16[16,16]{1,0:T(8,128)(2,1)S(1)} convert(s32[16,16]{1,0:T(8,128)} %param.10) | non-fusion elementwise | flops 256 | bytes 1536 | tf_op jit(solution)/shard_map/convert.1
  2.0 0.7 %convert.18 = bf16[16,32]{1,0:T(8,128)(2,1)S(1)} convert(s32[16,32]{1,0:T(8,128)} %param.14) | non-fusion elementwise | flops 512 | bytes 3072 | tf_op jit(solution)/shard_map/convert.3
  2.7 0.7 %convert.19 = bf16[16,32]{1,0:T(8,128)(2,1)S(1)} convert(s32[16,32]{1,0:T(8,128)} %param.15) | non-fusion elementwise | flops 512 | bytes 3072 | tf_op jit(solution)/shard_map/convert.4
  3.4 0.7 %convert.17 = bf16[16,32]{1,0:T(8,128)(2,1)S(1)} convert(s32[16,32]{1,0:T(8,128)} %dev_ref.1) | non-fusion elementwise | flops 512 | bytes 3072 | tf_op jit(solution)/shard_map/convert.2
  4.1 0.7 %concatenate.4.code_ref = bf16[16,128]{1,0:T(8,128)(2,1)} concatenate(bf16[16,16]{1,0:T(8,128)(2,1)S(1)} %convert.15, bf16[16,16]{1,0:T(8,128)(2,1)S(1)} %convert.16, bf16[16,32]{1,0:T(8,128)(2,1)S(1)} %convert.17, bf16[16,32]{1,0:T(8,128)(2,1)S(1)} %convert.18, bf16[16,32]{1,0:T(8,128)(2,1)S(1)} %convert.19), dimensions={1} | concatenate | bytes 8192 | tf_op jit(solution)/shard_map/concatenate | solution.py:280
  4.8 29.0 %gather.1 = (bf16[2,2,2,4,16,1280]{5,4,3,2,1,0:T(8,128)(2,1)}, bf16[2,2,2,4,16,1152]{5,4,3,2,1,0:T(8,128)(2,1)}) custom-call(bf16[16,2048]{1,0:T(8,128)(2,1)} %q_ref.1, bf16[16,128]{1,0:T(8,128)(2,1)} %concatenate.4.code_ref), custom_call_target="tpu_custom_call" | custom-call | tf_op jit(solution)/shard_map/gather/pallas_call | solution.py:286
  33.8 13.4 %score.1.src_ref = f32[32,8,128]{2,1,0:T(8,128)} custom-call(bf16[512,1280]{1,0:T(8,128)(2,1)} %bitcast.2, bf16[512,1152]{1,0:T(8,128)(2,1)} %bitcast.3, s32[16]{0:T(128)} %len_ref.1, bf16[16,256,2048]{2,1,0:T(8,128)(2,1)} %docs_ref.1), custom_call_target="tpu_custom_call" | custom-call | tf_op jit(solution)/shard_map/score/pallas_call | solution.py:305
  47.3 12.1 %exchange.1.got_ref = f32[32,8,128]{2,1,0:T(8,128)} custom-call(f32[32,8,128]{2,1,0:T(8,128)} %score.1.src_ref), custom_call_target="tpu_custom_call" | custom-call | tf_op jit(solution)/shard_map/exchange/pallas_call | solution.py:320
  59.4 2.3 %merge.1 = (f32[16,32]{1,0:T(8,128)}, f32[16,32]{1,0:T(8,128)}) custom-call(f32[32,8,128]{2,1,0:T(8,128)} %exchange.1.got_ref, s32[16,32]{1,0:T(8,128)} %dev_ref.1), custom_call_target="tpu_custom_call" | custom-call | tf_op jit(solution)/shard_map/merge/pallas_call | solution.py:333
where the time goes:
time: 62.1 us; the launch traced here: 61.7 us
  Pallas kernels  56.8 us (91%)
  other arithmetic  3.5 us (6%)
  local copies, waits for them, and re-layouts  0.68 us (1%)
  between operations  0.66 us (1%)
    pallas_call x1, Pallas kernels, shards(): pl.pallas_call(functools.partial(gather_kernel, split), out_shape=tuple((...  29 us
    pallas_call x1, Pallas kernels, shards(): pl.pallas_call(functools.partial(score_kernel, probes, shorts), out_shape...  13.4 us
    pallas_call x1, Pallas kernels, shards(): pl.pallas_call(exchange_kernel, out_shape=jax.ShapeDtypeStruct(returned.s...  12.1 us
    another operation x5, other arithmetic  3.5 us
    pallas_call x1, Pallas kernels, shards(): pl.pallas_call(merge_kernel, out_shape=(jax.ShapeDtypeStruct((query_rows,...  2.25 us

commit v1 on v0

v1 whole, which is shorter than its diff:
```python
import functools

import jax
import jax.numpy as jnp
from jax import lax
from jax.experimental import pallas as pl
from jax.experimental.pallas import tpu as pltpu
from jax.sharding import PartitionSpec as P

PREFIX = 256
TOPK = 32
SHORT_ROWS = 96
AXES = ("gx", "gy")
LANES = 128
TILE = 256
WIDTH = 256
NT = (((1,), (1,)), ((), ()))
MESH = pl.DeviceIdType.MESH


def row_norm(values):
    return jnp.sqrt(1.0 + jnp.sum(values * values, axis=1, keepdims=True))


def sort_pairs(n):
    p = 1
    while p < n:
        k = p
        while k >= 1:
            for j in range(k % p, n - k, 2 * k):
                for i in range(min(k, n - j - k)):
                    if (i + j) // (2 * p) == (i + j + k) // (2 * p):
                        yield i + j, i + j + k
            k //= 2
        p *= 2


def sort_desc(v):
    v = list(v)
    for a, b in sort_pairs(len(v)):
        v[a], v[b] = jnp.maximum(v[a], v[b]), jnp.minimum(v[a], v[b])
    return v


def bitonic_desc(v):
    n = len(v)
    step = n // 2
    while step:
        for i in range(n):
            if not i & step:
                v[i], v[i + step] = jnp.maximum(v[i], v[i + step]), jnp.minimum(v[i], v[i + step])
        step //= 2
    return v


def merge_top(a, b):
    n = len(a)
    if n < TOPK:
        return bitonic_desc(a + b[::-1])
    return bitonic_desc([jnp.maximum(a[i], b[n - 1 - i]) for i in range(n)])


def search_kernel(
    q_hbm, pd_hbm, pl_hbm, sd_hbm, sl_hbm, sr_hbm, len_ref, docs_hbm, top_ref, short_ref, *scratch,
):
    chunks = q_hbm.shape[1] // WIDTH
    gathered = scratch[:chunks]
    (queries, pd, plist, sd, sl, sr, pre_docs, top_docs, unit, spots, chosen, result,
     ret, got, acc, part_ret, part_got, load_sem, send_sem, line_recv, cube_recv,
     top_sem, part_sem) = scratch[chunks:]
    gx, gy = lax.axis_index("gx"), lax.axis_index("gy")
    line = lax.axis_size("gy")
    bits = (lax.axis_size("gx") - 1).bit_length()
    ranks = 1 << bits
    lists, rows, full = docs_hbm.shape
    query_rows = q_hbm.shape[0]
    probes, shorts = pd.shape[1], sd.shape[1]
    count = ranks * line
    total = count * query_rows
    tiles = total // TILE
    per_tile = TILE // query_rows
    per_lane = LANES // query_rows
    packed = query_rows * TOPK // LANES
    me = (gx * line + gy).astype(jnp.float32)

    def cross(r):
        there = gx
        for b in range(bits):
            if r >> b & 1:
                there = there + (1 - 2 * ((gx // (1 << b)) % 2)) * (1 << b)
        return there

    def slot(r, k):
        return ((r & 1) * (ranks // 2) + (r >> 1)) * line + k

    places = sorted((slot(r, k), r, k) for r in range(ranks) for k in range(line))
    across = [cross(r) for r in range(ranks)]

    barrier = pltpu.get_barrier_semaphore()
    for k in range(1, line):
        pl.semaphore_signal(barrier, inc=1, device_id=(gx, (gy + k) % line), device_id_type=MESH)
    for b in range(bits):
        pl.semaphore_signal(barrier, inc=1, device_id=(across[1 << b], gy), device_id_type=MESH)

    first = pltpu.make_async_copy(q_hbm.at[:, pl.ds(0, WIDTH)], gathered[0].at[0, :, pl.ds(0, WIDTH)], load_sem.at[0])
    first.start()
    small = [
        pltpu.make_async_copy(src, dst, load_sem.at[1 + i])
        for i, (src, dst) in enumerate([(pd_hbm, pd), (pl_hbm, plist), (sd_hbm, sd), (sl_hbm, sl), (sr_hbm, sr)])
    ]
    for copy in small:
        copy.start()
    whole = pltpu.make_async_copy(q_hbm, queries, load_sem.at[6])
    whole.start()
    pre_copy = pltpu.make_async_copy(docs_hbm.at[:, :, pl.ds(0, PREFIX)], pre_docs, load_sem.at[7])
    top_copy = pltpu.make_async_copy(docs_hbm.at[:, pl.ds(0, SHORT_ROWS), :], top_docs, load_sem.at[8])
    pre_copy.start()
    top_copy.start()
    for copy in small:
        copy.wait()
    codes = jnp.concatenate([x[...].astype(jnp.float32) for x in (pd, plist, sd, sl, sr)], axis=1)
    gathered[0][0, :, WIDTH:] = codes.astype(jnp.bfloat16)
    whole.wait()
    values = queries[...].astype(jnp.float32)
    norm = row_norm(values)
    for c in range(1, chunks):
        gathered[c][0] = (values[:, c * WIDTH:(c + 1) * WIDTH] / norm).astype(jnp.bfloat16)
    first.wait()
    pl.semaphore_wait(barrier, line - 1 + bits)

    def order(c):
        inner = list(range(1, bits))
        return inner if c % 2 == 0 else inner[::-1]

    def push(c, source, target, n, recv, device):
        pltpu.make_async_remote_copy(
            src_ref=gathered[c].at[pl.ds(source, n)], dst_ref=gathered[c].at[pl.ds(target, n)],
            send_sem=send_sem.at[c], recv_sem=recv, device_id=device, device_id_type=MESH,
        ).start()

    def pushes(c, r, k, n, stage):
        for b in order(c)[stage:]:
            push(c, slot(r, k), slot(r | 1 << b, k), n, cube_recv.at[c, b], (across[1 << b], gy))

    def arrived(ref, n, sem):
        part = ref.at[pl.ds(0, n)]
        pltpu.make_async_copy(part, part, sem).wait()

    def begin(c):
        for k in range(1, line):
            push(c, 0, k, 1, line_recv.at[c], (gx, (gy + k) % line))
        pushes(c, 0, 0, 1, 0)

    def relay(c, stage):
        inner = order(c)
        if stage == 0:
            arrived(gathered[c], line - 1, line_recv.at[c])
            pushes(c, 0, 1, line - 1, 0)
        else:
            b = inner[stage - 1]
            free = inner[:stage - 1]
            arrived(gathered[c], line << len(free), cube_recv.at[c, b])
            for pick in range(1 << len(free)):
                r = 1 << b
                for i, f in enumerate(free):
                    if pick >> i & 1:
                        r |= 1 << f
                pushes(c, r, 0, line, stage)
        if stage == len(inner):
            push(c, 0, count // 2, count // 2, cube_recv.at[c, 0], (across[1], gy))

    def rows_of(c, t, lo, hi):
        return gathered[c][t * per_tile:(t + 1) * per_tile, :, lo:hi].reshape(TILE, hi - lo)

    def give_tops(t):
        lane = lax.broadcasted_iota(jnp.int32, (8, LANES), 1)
        for u in range(TILE // LANES):
            turned = jnp.transpose(result[:, u * LANES:(u + 1) * LANES])
            for i in range(per_lane):
                low = turned[i * query_rows:i * query_rows + 8]
                high = pltpu.roll(turned[i * query_rows + 8:(i + 1) * query_rows], 64, 1)
                pair = jnp.where(lane < 64, low, high)
                swapped = pltpu.roll(pltpu.roll(pair, 4, 0), TOPK, 1)
                message = jnp.where(lane % 64 < TOPK, pair, swapped)[:packed]
                s, r, k = places[t * per_tile + u * per_lane + i]
                if s == 0:
                    got[0] = message
                    continue
                ret[s] = message
                pltpu.make_async_remote_copy(
                    src_ref=ret.at[s], dst_ref=got.at[s], send_sem=top_sem.at[0], recv_sem=top_sem.at[1],
                    device_id=(across[r], (gy + line - k) % line), device_id_type=MESH,
                ).start()

    def prefix(t):
        lanes = slice(t * TILE, (t + 1) * TILE)
        raw = rows_of(0, t, 0, PREFIX).astype(jnp.float32)
        unit[lanes, :] = (raw / row_norm(raw)).astype(jnp.bfloat16)
        turned = jnp.transpose(rows_of(0, t, WIDTH, WIDTH + LANES).astype(jnp.float32))
        p_dev, p_list = turned[:probes], turned[probes:2 * probes]
        base = 2 * probes
        s_dev, s_list, s_row = (turned[base + i * shorts:base + (i + 1) * shorts] for i in range(3))
        probed = jnp.sum(jnp.where(p_dev == me, p_list + 1.0, 0.0), axis=0, keepdims=True).astype(jnp.int32) - 1
        at = s_list * SHORT_ROWS + s_row + 1.0
        wanted = jnp.sum(jnp.where(s_dev == me, at, 0.0), axis=0, keepdims=True).astype(jnp.int32) - 1
        spots[0:1, lanes] = wanted
        chunk = 32

        @pl.loop(0, rows // chunk)
        def _(c):
            start = pl.multiple_of(c * chunk, chunk)
            docs = pre_docs[:, pl.ds(start, chunk), :].reshape(lists * chunk, PREFIX)
            scores = lax.dot_general(docs, unit[lanes, :], NT, preferred_element_type=jnp.float32)
            place = lax.broadcasted_iota(jnp.int32, (chunk, TILE), 0) + start
            value = jnp.full((chunk, TILE), -jnp.inf, jnp.float32)
            for l in range(lists):
                limit = jnp.where(probed == l, len_ref[l], 0)
                value = jnp.where(place < limit, scores[l * chunk:(l + 1) * chunk], value)
            chosen[pl.ds(start, chunk), :] = value

        @pl.loop(0, TILE // LANES)
        def _(u):
            spot = pl.ds(pl.multiple_of(u * LANES, LANES), LANES)
            v = [chosen[pl.ds(8 * i, 8), spot] for i in range(rows // 8)]
            parts = [sort_desc(v[i:i + TOPK]) for i in range(0, len(v), TOPK)]
            v = functools.reduce(merge_top, parts)
            for shift in (4, 2, 1):
                v = merge_top(v, [pltpu.roll(x, shift, 0) for x in v])
            sub = lax.broadcasted_iota(jnp.int32, (8, LANES), 0)
            for a in range(TOPK // 8):
                one = v[8 * a]
                for s in range(1, 8):
                    one = jnp.where(sub == s, v[8 * a + s], one)
                result[pl.ds(8 * a, 8), spot] = one

        give_tops(t)

    group = 4

    def rescore(c, t):
        lanes = slice(t * TILE, (t + 1) * TILE)
        block = rows_of(c, t, 0, WIDTH)
        wanted = spots[0:1, lanes]
        place = lax.broadcasted_iota(jnp.int32, (SHORT_ROWS, TILE), 0)
        kind = 0 if c == 0 else 1

        def step(g, total_acc):
            docs = top_docs[pl.ds(g * group, group), :, c * WIDTH:(c + 1) * WIDTH].reshape(group * SHORT_ROWS, WIDTH)
            scores = lax.dot_general(docs, block, NT, preferred_element_type=jnp.float32)
            for j in range(group):
                hit = place == wanted - (g * group + j) * SHORT_ROWS
                part = jnp.where(hit, scores[j * SHORT_ROWS:(j + 1) * SHORT_ROWS], 0.0)
                total_acc = total_acc + jnp.sum(part.reshape(SHORT_ROWS // 8, 8, TILE), axis=0)
            return total_acc

        before = jnp.zeros((8, TILE), jnp.float32) if c < 2 else acc[kind, :, lanes]
        acc[kind, :, lanes] = lax.fori_loop(0, lists // group, step, before)

    def work(c):
        if c == 0:
            pre_copy.wait()
            for t in range(tiles):
                prefix(t)
            top_copy.wait()
        for t in range(tiles):
            rescore(c, t)

    for c in range(chunks):
        begin(c)
    depth = bits + 1
    for wave in range(chunks + depth):
        for stage in range(depth, -1, -1):
            c = wave - stage
            if not 0 <= c < chunks:
                continue
            if stage < bits:
                relay(c, stage)
            elif stage == bits:
                arrived(gathered[c], count // 2, cube_recv.at[c, 0])
                work(c)

    for kind in range(2):
        sums = jnp.sum(acc[kind], axis=0, keepdims=True)
        for g in range(total // LANES):
            part_ret[g, kind:kind + 1, :] = sums[:, g * LANES:(g + 1) * LANES]
    part_got[0] = part_ret[0]
    for s, r, k in places[1:]:
        pltpu.make_async_remote_copy(
            src_ref=part_ret.at[s // per_lane], dst_ref=part_got.at[s], send_sem=part_sem.at[0],
            recv_sem=part_sem.at[1], device_id=(across[r], (gy + line - k) % line), device_id_type=MESH,
        ).start()

    arrived(got, count - 1, top_sem.at[1])
    v = [jnp.concatenate([got[i], got[i + 1]], axis=0) for i in range(0, count, 2)]
    parts = [sort_desc(v[i:i + TOPK]) for i in range(0, len(v), TOPK)]
    best = functools.reduce(merge_top, parts)
    best = merge_top(best, [pltpu.roll(x, 4, 0) for x in best])
    shift = TOPK // 2
    while shift:
        best = merge_top(best, [pltpu.roll(x, LANES - shift, 1) for x in best])
        shift //= 2
    lane = lax.broadcasted_iota(jnp.int32, (8, LANES), 1)
    out = best[0]
    for i in range(1, TOPK):
        out = jnp.where(lane % TOPK == i, pltpu.roll(best[i], i, 1), out)
    for g in range(LANES // TOPK):
        moved = out if g == 0 else pltpu.roll(out, LANES - g * TOPK, 1)
        top_ref[g * packed:(g + 1) * packed, :] = moved[:packed, :TOPK]

    arrived(part_got, count - 1, part_sem.at[1])
    lane = lax.broadcasted_iota(jnp.int32, (count, LANES), 1)
    owner = lax.broadcasted_iota(jnp.int32, (count, LANES), 0) % per_lane
    sums = []
    for kind in range(2):
        kept = jnp.where(lane // query_rows == owner, part_got[:, kind, :], 0.0)
        sums.append(jnp.sum(jnp.transpose(kept).reshape(per_lane, query_rows, count), axis=0))
    rescored = sums[0] / norm + sums[1]
    dev = sd[...]
    picked = jnp.zeros((query_rows, shorts), jnp.float32)
    for s, r, k in places:
        there = across[r] * line + (gy + k) % line
        picked = jnp.where(dev == there, rescored[:, s:s + 1], picked)
    short_ref[...] = picked

    for c in range(chunks):
        arrived(gathered[c], count - 1, send_sem.at[c])
    arrived(got, count - 1, top_sem.at[0])
    arrived(part_got, count - 1, part_sem.at[0])


def shards(queries, probe_dev, probe_list, documents, lengths, short_dev, short_list, short_row):
    count = lax.axis_size(AXES)
    lists, rows, full = documents.shape
    query_rows = queries.shape[0]
    probes, shorts = probe_dev.shape[1], short_dev.shape[1]
    total = count * query_rows
    chunks = full // WIDTH
    bits = (lax.axis_size("gx") - 1).bit_length()
    packed = query_rows * TOPK // LANES
    extra = 2 * probes + 3 * shorts
    vmem = pl.BlockSpec(memory_space=pltpu.VMEM)
    hbm = pl.BlockSpec(memory_space=pl.ANY)
    dma = pltpu.SemaphoreType.DMA
    return pl.pallas_call(
        search_kernel,
        out_shape=(
            jax.ShapeDtypeStruct((query_rows, TOPK), jnp.float32),
            jax.ShapeDtypeStruct((query_rows, shorts), jnp.float32),
        ),
        in_specs=[hbm] * 6 + [pl.BlockSpec(memory_space=pltpu.SMEM), hbm],
        out_specs=(vmem, vmem),
        scratch_shapes=[
            pltpu.VMEM((count, query_rows, WIDTH + (extra if c == 0 else 0)), jnp.bfloat16) for c in range(chunks)
        ] + [
            pltpu.VMEM((query_rows, full), jnp.bfloat16),
            pltpu.VMEM((query_rows, probes), jnp.int32),
            pltpu.VMEM((query_rows, probes), jnp.int32),
            pltpu.VMEM((query_rows, shorts), jnp.int32),
            pltpu.VMEM((query_rows, shorts), jnp.int32),
            pltpu.VMEM((query_rows, shorts), jnp.int32),
            pltpu.VMEM((lists, rows, PREFIX), jnp.bfloat16),
            pltpu.VMEM((lists, SHORT_ROWS, full), jnp.bfloat16),
            pltpu.VMEM((total, PREFIX), jnp.bfloat16),
            pltpu.VMEM((8, total), jnp.int32),
            pltpu.VMEM((rows, TILE), jnp.float32),
            pltpu.VMEM((LANES, TILE), jnp.float32),
            pltpu.VMEM((count, packed, LANES), jnp.float32),
            pltpu.VMEM((count, packed, LANES), jnp.float32),
            pltpu.VMEM((2, 8, total), jnp.float32),
            pltpu.VMEM((total // LANES, 2, LANES), jnp.float32),
            pltpu.VMEM((count, 2, LANES), jnp.float32),
            dma((9,)),
            dma((chunks,)),
            dma((chunks,)),
            dma((chunks, bits)),
            dma((2,)),
            dma((2,)),
        ],
        compiler_params=pltpu.CompilerParams(
            collective_id=0, has_side_effects=True, vmem_limit_bytes=60 * 1024 * 1024
        ),
        name="search",
    )(queries, probe_dev, probe_list, short_dev, short_list, short_row, lengths, documents)


def solution(mesh):
    one = P(AXES, None)
    in_specs = (one, one, one, P(AXES, None, None), P(AXES), one, one, one)
    return jax.shard_map(shards, mesh=mesh, in_specs=in_specs, out_specs=(one, one), check_vma=False)
```

time: 62.1 us -> 57.9 us (0.932)
  other arithmetic: 3.5 us -> 0 us
  Pallas kernels: 56.8 us -> 54.4 us
  local copies, waits for them, and re-layouts: 0.68 us -> 2.59 us
    another operation x5 -> x0, other arithmetic: 3.5 us -> none
    unnamed x0 -> x2, local copies, waits for them, and re-layouts: none -> 2.59 us
    pallas_call x4 -> x1, Pallas kernels: 56.8 us -> 54.4 us  [shards(): pl.pallas_call(search_kernel, out_shape=(jax.ShapeDtypeStruct((query_rows...]
    concatenate x1 -> x0, local copies, waits for them, and re-layouts: 0.68 us -> none  [shards(): jnp.concatenate([probe_dev, probe_list, short_dev, short_list, short_row]...]
where the time goes in v1:
time: 57.9 us; the launch traced here: 57.7 us
  Pallas kernels  54.4 us (94%)
  local copies, waits for them, and re-layouts  2.59 us (4%)
  between operations  0.64 us (1%)
    pallas_call x1, Pallas kernels, shards(): pl.pallas_call(search_kernel, out_shape=(jax.ShapeDtypeStruct((query_rows...  54.4 us
    unnamed x2, local copies, waits for them, and re-layouts  2.59 us

profile of v1, /device:TPU:0, one launch (start us, length us, event | category | flops | bytes accessed | tf_op | source)
XLA Modules:
  0.0 57.7 jit_solution(12035918599188306137)
XLA Ops:
  0.6 54.4 %search.1 = (f32[16,32]{1,0:T(8,128)}, f32[16,32]{1,0:T(8,128)}) custom-call(bf16[16,2048]{1,0:T(8,128)(2,1)} %q_hbm.1, s32[16,16]{1,0:T(8,128)} %pd_hbm.1, s32[16,16]{1,0:T(8,128)} %pl_hbm.1, s32[16,32]{1,0:T(8,128)} %sd_hbm.1, s32[16,32]{1,0:T(8,128)} %sl_hbm.1, s32[16,32]{1,0:T(8,128)} %sr_hbm.1, s32[16]{0:T(128)} %len_ref.1, bf16[16,256,2048]{2,1,0:T(8,128)(2,1)} %docs_hbm.1), custom_call_target="tpu_custom_call" | custom-call | tf_op jit(solution)/shard_map/search/pallas_call | solution.py:344
  55.1 1.3 %copy.12 = f32[16,32]{1,0:T(8,128)} copy(f32[16,32]{1,0:T(8,128)} %get-tuple-element.4) | data formatting | bytes 4096
  56.4 1.3 %copy.13 = f32[16,32]{1,0:T(8,128)} copy(f32[16,32]{1,0:T(8,128)} %get-tuple-element.5) | data formatting | bytes 4096

commit v2 on v1

--- a/solution.py
+++ b/solution.py
@@ -13,7 +13,6 @@
 AXES = ("gx", "gy")
 LANES = 128
 TILE = 256
-WIDTH = 256
 NT = (((1,), (1,)), ((), ()))
 MESH = pl.DeviceIdType.MESH
 
@@ -60,13 +59,21 @@
     return bitonic_desc([jnp.maximum(a[i], b[n - 1 - i]) for i in range(n)])
 
 
+def column_cuts(full):
+    cuts = [0, PREFIX]
+    while full - cuts[-1] > 2 * PREFIX:
+        cuts.append(cuts[-1] + 2 * PREFIX)
+    return cuts + [full]
+
+
 def search_kernel(
-    q_hbm, pd_hbm, pl_hbm, sd_hbm, sl_hbm, sr_hbm, len_ref, docs_hbm, top_ref, short_ref, *scratch,
+    q_hbm, pd_hbm, pl_hbm, sd_hbm, sl_hbm, sr_hbm, len_ref, docs_hbm, out_ref, *scratch,
 ):
-    chunks = q_hbm.shape[1] // WIDTH
+    cuts = column_cuts(q_hbm.shape[1])
+    chunks = len(cuts) - 1
     gathered = scratch[:chunks]
     (queries, pd, plist, sd, sl, sr, pre_docs, top_docs, unit, spots, chosen, result,
-     ret, got, acc, part_ret, part_got, load_sem, send_sem, line_recv, cube_recv,
+     ret, got, acc, part_ret, part_got, load_sem, send_sem, line_recv, plane_recv, core_recv,
      top_sem, part_sem) = scratch[chunks:]
     gx, gy = lax.axis_index("gx"), lax.axis_index("gy")
     line = lax.axis_size("gy")
@@ -99,10 +106,10 @@
     barrier = pltpu.get_barrier_semaphore()
     for k in range(1, line):
         pl.semaphore_signal(barrier, inc=1, device_id=(gx, (gy + k) % line), device_id_type=MESH)
-    for b in range(bits):
-        pl.semaphore_signal(barrier, inc=1, device_id=(across[1 << b], gy), device_id_type=MESH)
-
-    first = pltpu.make_async_copy(q_hbm.at[:, pl.ds(0, WIDTH)], gathered[0].at[0, :, pl.ds(0, WIDTH)], load_sem.at[0])
+    for r in [1, *range(2, ranks, 2)]:
+        pl.semaphore_signal(barrier, inc=1, device_id=(across[r], gy), device_id_type=MESH)
+
+    first = pltpu.make_async_copy(q_hbm.at[:, pl.ds(0, PREFIX)], gathered[0].at[0, :, pl.ds(0, PREFIX)], load_sem.at[0])
     first.start()
     small = [
         pltpu.make_async_copy(src, dst, load_sem.at[1 + i])
@@ -119,18 +126,10 @@
     for copy in small:
         copy.wait()
     codes = jnp.concatenate([x[...].astype(jnp.float32) for x in (pd, plist, sd, sl, sr)], axis=1)
-    gathered[0][0, :, WIDTH:] = codes.astype(jnp.bfloat16)
-    whole.wait()
-    values = queries[...].astype(jnp.float32)
-    norm = row_norm(values)
-    for c in range(1, chunks):
-        gathered[c][0] = (values[:, c * WIDTH:(c + 1) * WIDTH] / norm).astype(jnp.bfloat16)
+    gathered[0][0, :, PREFIX:] = codes.astype(jnp.bfloat16)
     first.wait()
-    pl.semaphore_wait(barrier, line - 1 + bits)
-
-    def order(c):
-        inner = list(range(1, bits))
-        return inner if c % 2 == 0 else inner[::-1]
+    pl.semaphore_wait(barrier, line + ranks // 2 - 1)
+    plane = [r for r in range(2, ranks, 2)]
 
     def push(c, source, target, n, recv, device):
         pltpu.make_async_remote_copy(
@@ -138,10 +137,6 @@
             send_sem=send_sem.at[c], recv_sem=recv, device_id=device, device_id_type=MESH,
         ).start()
 
-    def pushes(c, r, k, n, stage):
-        for b in order(c)[stage:]:
-            push(c, slot(r, k), slot(r | 1 << b, k), n, cube_recv.at[c, b], (across[1 << b], gy))
-
     def arrived(ref, n, sem):
         part = ref.at[pl.ds(0, n)]
         pltpu.make_async_copy(part, part, sem).wait()
@@ -149,30 +144,34 @@
     def begin(c):
         for k in range(1, line):
             push(c, 0, k, 1, line_recv.at[c], (gx, (gy + k) % line))
-        pushes(c, 0, 0, 1, 0)
-
-    def relay(c, stage):
-        inner = order(c)
-        if stage == 0:
-            arrived(gathered[c], line - 1, line_recv.at[c])
-            pushes(c, 0, 1, line - 1, 0)
-        else:
-            b = inner[stage - 1]
-            free = inner[:stage - 1]
-            arrived(gathered[c], line << len(free), cube_recv.at[c, b])
-            for pick in range(1 << len(free)):
-                r = 1 << b
-                for i, f in enumerate(free):
-                    if pick >> i & 1:
-                        r |= 1 << f
-                pushes(c, r, 0, line, stage)
-        if stage == len(inner):
-            push(c, 0, count // 2, count // 2, cube_recv.at[c, 0], (across[1], gy))
+        for r in plane:
+            push(c, 0, slot(r, 0), 1, plane_recv.at[c], (across[r], gy))
+
+    def spread(c):
+        arrived(gathered[c], line - 1, line_recv.at[c])
+        for r in plane:
+            push(c, 1, slot(r, 1), line - 1, plane_recv.at[c], (across[r], gy))
+
+    def share(c):
+        arrived(gathered[c], len(plane) * line, plane_recv.at[c])
+        push(c, 0, count // 2, count // 2, core_recv.at[c], (across[1], gy))
+
+    def shared(c):
+        arrived(gathered[c], count // 2, core_recv.at[c])
+
+    begin(0)
+    whole.wait()
+    values = queries[...].astype(jnp.float32)
+    norm = row_norm(values)
+    for c in range(1, chunks):
+        gathered[c][0] = (values[:, cuts[c]:cuts[c + 1]] / norm).astype(jnp.bfloat16)
+    for c in range(1, chunks):
+        begin(c)
 
     def rows_of(c, t, lo, hi):
         return gathered[c][t * per_tile:(t + 1) * per_tile, :, lo:hi].reshape(TILE, hi - lo)
 
-    def give_tops(t):
+    def pack_tops(t):
         lane = lax.broadcasted_iota(jnp.int32, (8, LANES), 1)
         for u in range(TILE // LANES):
             turned = jnp.transpose(result[:, u * LANES:(u + 1) * LANES])
@@ -182,21 +181,37 @@
                 pair = jnp.where(lane < 64, low, high)
                 swapped = pltpu.roll(pltpu.roll(pair, 4, 0), TOPK, 1)
                 message = jnp.where(lane % 64 < TOPK, pair, swapped)[:packed]
-                s, r, k = places[t * per_tile + u * per_lane + i]
+                s = t * per_tile + u * per_lane + i
                 if s == 0:
                     got[0] = message
-                    continue
-                ret[s] = message
-                pltpu.make_async_remote_copy(
-                    src_ref=ret.at[s], dst_ref=got.at[s], send_sem=top_sem.at[0], recv_sem=top_sem.at[1],
-                    device_id=(across[r], (gy + line - k) % line), device_id_type=MESH,
-                ).start()
+                else:
+                    ret[s] = message
+
+    def give(source, target, sems, some):
+        for s, r, k in places[some.start * per_tile:some.stop * per_tile]:
+            if s == 0:
+                continue
+            pltpu.make_async_remote_copy(
+                src_ref=source(s), dst_ref=target.at[s], send_sem=sems.at[0], recv_sem=sems.at[1],
+                device_id=(across[r], (gy + line - k) % line), device_id_type=MESH,
+            ).start()
+
+    def give_parts(some):
+        lanes = slice(some.start * TILE, some.stop * TILE)
+        first = some.start * TILE // LANES
+        for kind in range(2):
+            sums = jnp.sum(acc[kind, :, lanes], axis=0, keepdims=True)
+            for g in range(len(some) * TILE // LANES):
+                part_ret[first + g, kind:kind + 1, :] = sums[:, g * LANES:(g + 1) * LANES]
+        if some.start == 0:
+            part_got[0] = part_ret[0]
+        give(lambda s: part_ret.at[s // per_lane], part_got, part_sem, some)
 
     def prefix(t):
         lanes = slice(t * TILE, (t + 1) * TILE)
         raw = rows_of(0, t, 0, PREFIX).astype(jnp.float32)
         unit[lanes, :] = (raw / row_norm(raw)).astype(jnp.bfloat16)
-        turned = jnp.transpose(rows_of(0, t, WIDTH, WIDTH + LANES).astype(jnp.float32))
+        turned = jnp.transpose(rows_of(0, t, PREFIX, gathered[0].shape[2]).astype(jnp.float32))
         p_dev, p_list = turned[:probes], turned[probes:2 * probes]
         base = 2 * probes
         s_dev, s_list, s_row = (turned[base + i * shorts:base + (i + 1) * shorts] for i in range(3))
@@ -204,7 +219,7 @@
         at = s_list * SHORT_ROWS + s_row + 1.0
         wanted = jnp.sum(jnp.where(s_dev == me, at, 0.0), axis=0, keepdims=True).astype(jnp.int32) - 1
         spots[0:1, lanes] = wanted
-        chunk = 32
+        chunk = 128
 
         @pl.loop(0, rows // chunk)
         def _(c):
@@ -233,62 +248,53 @@
                     one = jnp.where(sub == s, v[8 * a + s], one)
                 result[pl.ds(8 * a, 8), spot] = one
 
-        give_tops(t)
-
-    group = 4
+        pack_tops(t)
 
     def rescore(c, t):
         lanes = slice(t * TILE, (t + 1) * TILE)
-        block = rows_of(c, t, 0, WIDTH)
+        width = cuts[c + 1] - cuts[c]
         wanted = spots[0:1, lanes]
         place = lax.broadcasted_iota(jnp.int32, (SHORT_ROWS, TILE), 0)
         kind = 0 if c == 0 else 1
-
-        def step(g, total_acc):
-            docs = top_docs[pl.ds(g * group, group), :, c * WIDTH:(c + 1) * WIDTH].reshape(group * SHORT_ROWS, WIDTH)
-            scores = lax.dot_general(docs, block, NT, preferred_element_type=jnp.float32)
-            for j in range(group):
-                hit = place == wanted - (g * group + j) * SHORT_ROWS
-                part = jnp.where(hit, scores[j * SHORT_ROWS:(j + 1) * SHORT_ROWS], 0.0)
-                total_acc = total_acc + jnp.sum(part.reshape(SHORT_ROWS // 8, 8, TILE), axis=0)
-            return total_acc
-
-        before = jnp.zeros((8, TILE), jnp.float32) if c < 2 else acc[kind, :, lanes]
-        acc[kind, :, lanes] = lax.fori_loop(0, lists // group, step, before)
-
-    def work(c):
-        if c == 0:
-            pre_copy.wait()
-            for t in range(tiles):
-                prefix(t)
-            top_copy.wait()
-        for t in range(tiles):
+        docs = top_docs[:, :, cuts[c]:cuts[c + 1]].reshape(lists * SHORT_ROWS, width)
+        scores = lax.dot_general(docs, rows_of(c, t, 0, width), NT, preferred_element_type=jnp.float32)
+        sums = jnp.zeros((8, TILE), jnp.float32) if c < 2 else acc[kind, :, lanes]
+        for j in range(lists):
+            hit = place == wanted - j * SHORT_ROWS
+            part = jnp.where(hit, scores[j * SHORT_ROWS:(j + 1) * SHORT_ROWS], 0.0)
+            sums = sums + jnp.sum(part.reshape(SHORT_ROWS // 8, 8, TILE), axis=0)
+        acc[kind, :, lanes] = sums
+
+    halves = (range(tiles // 2), range(tiles // 2, tiles))
+    for c in range(chunks):
+        spread(c)
+    share(0)
+    pre_copy.wait()
+    for t in halves[0]:
+        prefix(t)
+    shared(0)
+    for t in halves[1]:
+        prefix(t)
+    top_copy.wait()
+    for t in range(tiles):
+        rescore(0, t)
+    last = chunks - 1
+    share(1)
+    for c in range(1, chunks):
+        for t in halves[0]:
             rescore(c, t)
-
-    for c in range(chunks):
-        begin(c)
-    depth = bits + 1
-    for wave in range(chunks + depth):
-        for stage in range(depth, -1, -1):
-            c = wave - stage
-            if not 0 <= c < chunks:
-                continue
-            if stage < bits:
-                relay(c, stage)
-            elif stage == bits:
-                arrived(gathered[c], count // 2, cube_recv.at[c, 0])
-                work(c)
-
-    for kind in range(2):
-        sums = jnp.sum(acc[kind], axis=0, keepdims=True)
-        for g in range(total // LANES):
-            part_ret[g, kind:kind + 1, :] = sums[:, g * LANES:(g + 1) * LANES]
-    part_got[0] = part_ret[0]
-    for s, r, k in places[1:]:
-        pltpu.make_async_remote_copy(
-            src_ref=part_ret.at[s // per_lane], dst_ref=part_got.at[s], send_sem=part_sem.at[0],
-            recv_sem=part_sem.at[1], device_id=(across[r], (gy + line - k) % line), device_id_type=MESH,
-        ).start()
+        if c == last:
+            give_parts(halves[0])
+        elif c > 1:
+            share(c + 1)
+        if c == last - 2:
+            give(lambda s: ret.at[s], got, top_sem, range(tiles))
+        shared(c)
+        for t in halves[1]:
+            rescore(c, t)
+        if c == 1:
+            share(2)
+    give_parts(halves[1])
 
     arrived(got, count - 1, top_sem.at[1])
     v = [jnp.concatenate([got[i], got[i + 1]], axis=0) for i in range(0, count, 2)]
@@ -305,7 +311,7 @@
         out = jnp.where(lane % TOPK == i, pltpu.roll(best[i], i, 1), out)
     for g in range(LANES // TOPK):
         moved = out if g == 0 else pltpu.roll(out, LANES - g * TOPK, 1)
-        top_ref[g * packed:(g + 1) * packed, :] = moved[:packed, :TOPK]
+        out_ref[g * packed:(g + 1) * packed, :TOPK] = moved[:packed, :TOPK]
 
     arrived(part_got, count - 1, part_sem.at[1])
     lane = lax.broadcasted_iota(jnp.int32, (count, LANES), 1)
@@ -320,7 +326,7 @@
     for s, r, k in places:
         there = across[r] * line + (gy + k) % line
         picked = jnp.where(dev == there, rescored[:, s:s + 1], picked)
-    short_ref[...] = picked
+    out_ref[:, TOPK:] = picked
 
     for c in range(chunks):
         arrived(gathered[c], count - 1, send_sem.at[c])
@@ -334,23 +340,21 @@
     query_rows = queries.shape[0]
     probes, shorts = probe_dev.shape[1], short_dev.shape[1]
     total = count * query_rows
-    chunks = full // WIDTH
-    bits = (lax.axis_size("gx") - 1).bit_length()
+    cuts = column_cuts(full)
+    chunks = len(cuts) - 1
     packed = query_rows * TOPK // LANES
     extra = 2 * probes + 3 * shorts
     vmem = pl.BlockSpec(memory_space=pltpu.VMEM)
     hbm = pl.BlockSpec(memory_space=pl.ANY)
     dma = pltpu.SemaphoreType.DMA
-    return pl.pallas_call(
+    out = pl.pallas_call(
         search_kernel,
-        out_shape=(
-            jax.ShapeDtypeStruct((query_rows, TOPK), jnp.float32),
-            jax.ShapeDtypeStruct((query_rows, shorts), jnp.float32),
-        ),
+        out_shape=jax.ShapeDtypeStruct((query_rows, TOPK + shorts), jnp.float32),
         in_specs=[hbm] * 6 + [pl.BlockSpec(memory_space=pltpu.SMEM), hbm],
-        out_specs=(vmem, vmem),
+        out_specs=vmem,
         scratch_shapes=[
-            pltpu.VMEM((count, query_rows, WIDTH + (extra if c == 0 else 0)), jnp.bfloat16) for c in range(chunks)
+            pltpu.VMEM((count, query_rows, cuts[c + 1] - cuts[c] + (extra if c == 0 else 0)), jnp.bfloat16)
+            for c in range(chunks)
         ] + [
             pltpu.VMEM((query_rows, full), jnp.bfloat16),
             pltpu.VMEM((query_rows, probes), jnp.int32),
@@ -372,7 +376,8 @@
             dma((9,)),
             dma((chunks,)),
             dma((chunks,)),
-            dma((chunks, bits)),
+            dma((chunks,)),
+            dma((chunks,)),
             dma((2,)),
             dma((2,)),
         ],
@@ -381,6 +386,7 @@
         ),
         name="search",
     )(queries, probe_dev, probe_list, short_dev, short_list, short_row, lengths, documents)
+    return out[:, :TOPK], out[:, TOPK:]
 
 
 def solution(mesh):

time: 57.9 us -> 32.8 us (0.57)
  Pallas kernels: 54.4 us -> 30.5 us
  local copies, waits for them, and re-layouts: 2.59 us -> 1.45 us
    pallas_call x1, Pallas kernels: 54.4 us -> 30.5 us  [shards(): pl.pallas_call(search_kernel, out_shape=jax.ShapeDtypeStruct((query_rows,...]
    unnamed x2 -> x0, local copies, waits for them, and re-layouts: 2.59 us -> none
    slice x0 -> x1, local copies, waits for them, and re-layouts: none -> 1.45 us  [shards(): return (out[:, :TOPK], out[:, TOPK:])]
where the time goes in v2:
time: 32.8 us; the launch traced here: 32.6 us
  Pallas kernels  30.5 us (93%)
  local copies, waits for them, and re-layouts  1.45 us (4%)
  between operations  0.64 us (2%)
    pallas_call x1, Pallas kernels, shards(): pl.pallas_call(search_kernel, out_shape=jax.ShapeDtypeStruct((query_rows,...  30.5 us
    slice x1, local copies, waits for them, and re-layouts, shards(): return (out[:, :TOPK], out[:, TOPK:])  1.45 us

profile of v2, /device:TPU:0, one launch (start us, length us, event | category | flops | bytes accessed | tf_op | source)
XLA Modules:
  0.0 32.6 jit_solution(16361445946042676452)
XLA Ops:
  0.6 30.5 %search.1 = f32[16,64]{1,0:T(8,128)} custom-call(bf16[16,2048]{1,0:T(8,128)(2,1)} %q_hbm.1, s32[16,16]{1,0:T(8,128)} %pd_hbm.1, s32[16,16]{1,0:T(8,128)} %pl_hbm.1, s32[16,32]{1,0:T(8,128)} %sd_hbm.1, s32[16,32]{1,0:T(8,128)} %sl_hbm.1, s32[16,32]{1,0:T(8,128)} %sr_hbm.1, s32[16]{0:T(128)} %len_ref.1, bf16[16,256,2048]{2,1,0:T(8,128)(2,1)} %docs_hbm.1), custom_call_target="tpu_custom_call" | custom-call | tf_op jit(solution)/shard_map/search/pallas_call | solution.py:350
  31.2 1.4 %fusion = (f32[16,32]{1,0:T(8,128)}, f32[16,32]{1,0:T(8,128)}) fusion(f32[16,64]{1,0:T(8,128)} %search.1), kind=kLoop, calls=%fused_computation | loop fusion | bytes 8192 | tf_op jit(solution)/shard_map/slice | solution.py:389

commit v3 on v2

--- a/solution.py
+++ b/solution.py
@@ -73,7 +73,7 @@
     chunks = len(cuts) - 1
     gathered = scratch[:chunks]
     (queries, pd, plist, sd, sl, sr, pre_docs, top_docs, unit, spots, chosen, result,
-     ret, got, acc, part_ret, part_got, load_sem, send_sem, line_recv, plane_recv, core_recv,
+     ret, got, acc, part_ret, part_got, load_sem, docs_sem, send_sem, line_recv, plane_recv, core_recv,
      top_sem, part_sem) = scratch[chunks:]
     gx, gy = lax.axis_index("gx"), lax.axis_index("gy")
     line = lax.axis_size("gy")
@@ -109,37 +109,53 @@
     for r in [1, *range(2, ranks, 2)]:
         pl.semaphore_signal(barrier, inc=1, device_id=(across[r], gy), device_id_type=MESH)
 
-    first = pltpu.make_async_copy(q_hbm.at[:, pl.ds(0, PREFIX)], gathered[0].at[0, :, pl.ds(0, PREFIX)], load_sem.at[0])
-    first.start()
+    def columns(k):
+        return pl.ds(k * LANES, LANES)
+
+    head = PREFIX // LANES
+    firsts = [
+        pltpu.make_async_copy(q_hbm.at[:, columns(k)], gathered[0].at[k, 0], load_sem.at[7 + k]) for k in range(head)
+    ]
+    for copy in firsts:
+        copy.start()
     small = [
-        pltpu.make_async_copy(src, dst, load_sem.at[1 + i])
+        pltpu.make_async_copy(src, dst, load_sem.at[i])
         for i, (src, dst) in enumerate([(pd_hbm, pd), (pl_hbm, plist), (sd_hbm, sd), (sl_hbm, sl), (sr_hbm, sr)])
     ]
     for copy in small:
         copy.start()
-    whole = pltpu.make_async_copy(q_hbm, queries, load_sem.at[6])
+    whole = pltpu.make_async_copy(q_hbm, queries, load_sem.at[5])
     whole.start()
-    pre_copy = pltpu.make_async_copy(docs_hbm.at[:, :, pl.ds(0, PREFIX)], pre_docs, load_sem.at[7])
-    top_copy = pltpu.make_async_copy(docs_hbm.at[:, pl.ds(0, SHORT_ROWS), :], top_docs, load_sem.at[8])
-    pre_copy.start()
-    top_copy.start()
+    pre_copies = [
+        pltpu.make_async_copy(docs_hbm.at[:, :, columns(k)], pre_docs.at[k], docs_sem.at[k]) for k in range(head)
+    ]
+    top_copies = [
+        pltpu.make_async_copy(docs_hbm.at[:, pl.ds(0, SHORT_ROWS), columns(k)], top_docs.at[k - head], docs_sem.at[k])
+        for k in range(head, full // LANES)
+    ]
+    for copy in pre_copies + top_copies:
+        copy.start()
     for copy in small:
         copy.wait()
     codes = jnp.concatenate([x[...].astype(jnp.float32) for x in (pd, plist, sd, sl, sr)], axis=1)
-    gathered[0][0, :, PREFIX:] = codes.astype(jnp.bfloat16)
-    first.wait()
+    for k in range(head, gathered[0].shape[0]):
+        gathered[0][k, 0] = codes[:, (k - head) * LANES:(k - head + 1) * LANES].astype(jnp.bfloat16)
+    for copy in firsts:
+        copy.wait()
     pl.semaphore_wait(barrier, line + ranks // 2 - 1)
     plane = [r for r in range(2, ranks, 2)]
 
     def push(c, source, target, n, recv, device):
         pltpu.make_async_remote_copy(
-            src_ref=gathered[c].at[pl.ds(source, n)], dst_ref=gathered[c].at[pl.ds(target, n)],
+            src_ref=gathered[c].at[:, pl.ds(source, n)], dst_ref=gathered[c].at[:, pl.ds(target, n)],
             send_sem=send_sem.at[c], recv_sem=recv, device_id=device, device_id_type=MESH,
         ).start()
 
-    def arrived(ref, n, sem):
-        part = ref.at[pl.ds(0, n)]
+    def finish(part, sem):
         pltpu.make_async_copy(part, part, sem).wait()
+
+    def arrived(c, n, sem):
+        finish(gathered[c].at[:, pl.ds(0, n)], sem)
 
     def begin(c):
         for k in range(1, line):
@@ -148,28 +164,31 @@
             push(c, 0, slot(r, 0), 1, plane_recv.at[c], (across[r], gy))
 
     def spread(c):
-        arrived(gathered[c], line - 1, line_recv.at[c])
+        arrived(c, line - 1, line_recv.at[c])
         for r in plane:
             push(c, 1, slot(r, 1), line - 1, plane_recv.at[c], (across[r], gy))
 
     def share(c):
-        arrived(gathered[c], len(plane) * line, plane_recv.at[c])
+        arrived(c, len(plane) * line, plane_recv.at[c])
         push(c, 0, count // 2, count // 2, core_recv.at[c], (across[1], gy))
 
     def shared(c):
-        arrived(gathered[c], count // 2, core_recv.at[c])
+        arrived(c, count // 2, core_recv.at[c])
 
     begin(0)
     whole.wait()
     values = queries[...].astype(jnp.float32)
     norm = row_norm(values)
     for c in range(1, chunks):
-        gathered[c][0] = (values[:, cuts[c]:cuts[c + 1]] / norm).astype(jnp.bfloat16)
+        for k in range(gathered[c].shape[0]):
+            at = cuts[c] + k * LANES
+            gathered[c][k, 0] = (values[:, at:at + LANES] / norm).astype(jnp.bfloat16)
     for c in range(1, chunks):
         begin(c)
 
-    def rows_of(c, t, lo, hi):
-        return gathered[c][t * per_tile:(t + 1) * per_tile, :, lo:hi].reshape(TILE, hi - lo)
+    def rows_of(c, t, ks):
+        slots = slice(t * per_tile, (t + 1) * per_tile)
+        return jnp.concatenate([gathered[c][k, slots].reshape(TILE, LANES) for k in ks], axis=1)
 
     def pack_tops(t):
         lane = lax.broadcasted_iota(jnp.int32, (8, LANES), 1)
@@ -209,9 +228,9 @@
 
     def prefix(t):
         lanes = slice(t * TILE, (t + 1) * TILE)
-        raw = rows_of(0, t, 0, PREFIX).astype(jnp.float32)
+        raw = rows_of(0, t, range(head)).astype(jnp.float32)
         unit[lanes, :] = (raw / row_norm(raw)).astype(jnp.bfloat16)
-        turned = jnp.transpose(rows_of(0, t, PREFIX, gathered[0].shape[2]).astype(jnp.float32))
+        turned = jnp.transpose(rows_of(0, t, range(head, gathered[0].shape[0])).astype(jnp.float32))
         p_dev, p_list = turned[:probes], turned[probes:2 * probes]
         base = 2 * probes
         s_dev, s_list, s_row = (turned[base + i * shorts:base + (i + 1) * shorts] for i in range(3))
@@ -219,24 +238,28 @@
         at = s_list * SHORT_ROWS + s_row + 1.0
         wanted = jnp.sum(jnp.where(s_dev == me, at, 0.0), axis=0, keepdims=True).astype(jnp.int32) - 1
         spots[0:1, lanes] = wanted
-        chunk = 128
-
-        @pl.loop(0, rows // chunk)
-        def _(c):
-            start = pl.multiple_of(c * chunk, chunk)
-            docs = pre_docs[:, pl.ds(start, chunk), :].reshape(lists * chunk, PREFIX)
+        chunk = 32
+
+        order = [slice(r, r + chunk) for r in range(0, rows, chunk)]
+        limits = [jnp.where(probed == l, len_ref[l], 0) for l in range(lists)]
+        for part in (order[:len(order) // 2], order[len(order) // 2:]):
+            docs = jnp.concatenate([
+                jnp.concatenate([pre_docs[k, :, some].reshape(lists * chunk, LANES) for k in range(head)], axis=1)
+                for some in part
+            ], axis=0)
             scores = lax.dot_general(docs, unit[lanes, :], NT, preferred_element_type=jnp.float32)
-            place = lax.broadcasted_iota(jnp.int32, (chunk, TILE), 0) + start
-            value = jnp.full((chunk, TILE), -jnp.inf, jnp.float32)
-            for l in range(lists):
-                limit = jnp.where(probed == l, len_ref[l], 0)
-                value = jnp.where(place < limit, scores[l * chunk:(l + 1) * chunk], value)
-            chosen[pl.ds(start, chunk), :] = value
-
-        @pl.loop(0, TILE // LANES)
-        def _(u):
-            spot = pl.ds(pl.multiple_of(u * LANES, LANES), LANES)
-            v = [chosen[pl.ds(8 * i, 8), spot] for i in range(rows // 8)]
+            for i, some in enumerate(part):
+                place = lax.broadcasted_iota(jnp.int32, (chunk, TILE), 0) + some.start
+                value = jnp.full((chunk, TILE), -jnp.inf, jnp.float32)
+                for l in range(lists):
+                    at = (i * lists + l) * chunk
+                    value = jnp.where(place < limits[l], scores[at:at + chunk], value)
+                chosen[t, some, :] = value
+
+    def tops(t):
+        for u in range(TILE // LANES):
+            spot = slice(u * LANES, (u + 1) * LANES)
+            v = [chosen[t, 8 * i:8 * i + 8, spot] for i in range(rows // 8)]
             parts = [sort_desc(v[i:i + TOPK]) for i in range(0, len(v), TOPK)]
             v = functools.reduce(merge_top, parts)
             for shift in (4, 2, 1):
@@ -246,8 +269,7 @@
                 one = v[8 * a]
                 for s in range(1, 8):
                     one = jnp.where(sub == s, v[8 * a + s], one)
-                result[pl.ds(8 * a, 8), spot] = one
-
+                result[8 * a:8 * a + 8, spot] = one
         pack_tops(t)
 
     def rescore(c, t):
@@ -256,8 +278,10 @@
         wanted = spots[0:1, lanes]
         place = lax.broadcasted_iota(jnp.int32, (SHORT_ROWS, TILE), 0)
         kind = 0 if c == 0 else 1
-        docs = top_docs[:, :, cuts[c]:cuts[c + 1]].reshape(lists * SHORT_ROWS, width)
-        scores = lax.dot_general(docs, rows_of(c, t, 0, width), NT, preferred_element_type=jnp.float32)
+        ks = range(width // LANES)
+        tall = [pre_docs[k, :, :SHORT_ROWS] if c == 0 else top_docs[cuts[c] // LANES - head + k] for k in ks]
+        docs = jnp.concatenate([x.reshape(lists * SHORT_ROWS, LANES) for x in tall], axis=1)
+        scores = lax.dot_general(docs, rows_of(c, t, ks), NT, preferred_element_type=jnp.float32)
         sums = jnp.zeros((8, TILE), jnp.float32) if c < 2 else acc[kind, :, lanes]
         for j in range(lists):
             hit = place == wanted - j * SHORT_ROWS
@@ -269,34 +293,33 @@
     for c in range(chunks):
         spread(c)
     share(0)
-    pre_copy.wait()
+    for copy in pre_copies:
+        copy.wait()
     for t in halves[0]:
         prefix(t)
     shared(0)
+    for t in halves[0]:
+        tops(t)
     for t in halves[1]:
         prefix(t)
-    top_copy.wait()
+    share(1)
     for t in range(tiles):
         rescore(0, t)
-    last = chunks - 1
-    share(1)
+    for t in halves[1]:
+        tops(t)
+    for copy in top_copies:
+        copy.wait()
     for c in range(1, chunks):
-        for t in halves[0]:
+        if c + 1 < chunks:
+            share(c + 1)
+        shared(c)
+        for t in range(tiles):
             rescore(c, t)
-        if c == last:
-            give_parts(halves[0])
-        elif c > 1:
-            share(c + 1)
-        if c == last - 2:
+        if c == chunks - 3:
             give(lambda s: ret.at[s], got, top_sem, range(tiles))
-        shared(c)
-        for t in halves[1]:
-            rescore(c, t)
-        if c == 1:
-            share(2)
-    give_parts(halves[1])
-
-    arrived(got, count - 1, top_sem.at[1])
+    give_parts(range(tiles))
+
+    finish(got.at[pl.ds(0, count - 1)], top_sem.at[1])
     v = [jnp.concatenate([got[i], got[i + 1]], axis=0) for i in range(0, count, 2)]
     parts = [sort_desc(v[i:i + TOPK]) for i in range(0, len(v), TOPK)]
     best = functools.reduce(merge_top, parts)
@@ -313,7 +336,7 @@
         moved = out if g == 0 else pltpu.roll(out, LANES - g * TOPK, 1)
         out_ref[g * packed:(g + 1) * packed, :TOPK] = moved[:packed, :TOPK]
 
-    arrived(part_got, count - 1, part_sem.at[1])
+    finish(part_got.at[pl.ds(0, count - 1)], part_sem.at[1])
     lane = lax.broadcasted_iota(jnp.int32, (count, LANES), 1)
     owner = lax.broadcasted_iota(jnp.int32, (count, LANES), 0) % per_lane
     sums = []
@@ -329,9 +352,9 @@
     out_ref[:, TOPK:] = picked
 
     for c in range(chunks):
-        arrived(gathered[c], count - 1, send_sem.at[c])
-    arrived(got, count - 1, top_sem.at[0])
-    arrived(part_got, count - 1, part_sem.at[0])
+        arrived(c, count - 1, send_sem.at[c])
+    finish(got.at[pl.ds(0, count - 1)], top_sem.at[0])
+    finish(part_got.at[pl.ds(0, count - 1)], part_sem.at[0])
 
 
 def shards(queries, probe_dev, probe_list, documents, lengths, short_dev, short_list, short_row):
@@ -353,7 +376,9 @@
         in_specs=[hbm] * 6 + [pl.BlockSpec(memory_space=pltpu.SMEM), hbm],
         out_specs=vmem,
         scratch_shapes=[
-            pltpu.VMEM((count, query_rows, cuts[c + 1] - cuts[c] + (extra if c == 0 else 0)), jnp.bfloat16)
+            pltpu.VMEM(
+                ((cuts[c + 1] - cuts[c] + (extra if c == 0 else 0)) // LANES, count, query_rows, LANES), jnp.bfloat16
+            )
             for c in range(chunks)
         ] + [
             pltpu.VMEM((query_rows, full), jnp.bfloat16),
@@ -362,11 +387,11 @@
             pltpu.VMEM((query_rows, shorts), jnp.int32),
             pltpu.VMEM((query_rows, shorts), jnp.int32),
             pltpu.VMEM((query_rows, shorts), jnp.int32),
-            pltpu.VMEM((lists, rows, PREFIX), jnp.bfloat16),
-            pltpu.VMEM((lists, SHORT_ROWS, full), jnp.bfloat16),
+            pltpu.VMEM((PREFIX // LANES, lists, rows, LANES), jnp.bfloat16),
+            pltpu.VMEM(((full - PREFIX) // LANES, lists, SHORT_ROWS, LANES), jnp.bfloat16),
             pltpu.VMEM((total, PREFIX), jnp.bfloat16),
             pltpu.VMEM((8, total), jnp.int32),
-            pltpu.VMEM((rows, TILE), jnp.float32),
+            pltpu.VMEM((total // TILE, rows, TILE), jnp.float32),
             pltpu.VMEM((LANES, TILE), jnp.float32),
             pltpu.VMEM((count, packed, LANES), jnp.float32),
             pltpu.VMEM((count, packed, LANES), jnp.float32),
@@ -374,6 +399,7 @@
             pltpu.VMEM((total // LANES, 2, LANES), jnp.float32),
             pltpu.VMEM((count, 2, LANES), jnp.float32),
             dma((9,)),
+            dma((full // LANES,)),
             dma((chunks,)),
             dma((chunks,)),
             dma((chunks,)),

time: 32.8 us -> 31 us (0.945)
  Pallas kernels: 30.5 us -> 28.7 us
    pallas_call x1, Pallas kernels: 30.5 us -> 28.7 us  [shards(): pl.pallas_call(search_kernel, out_shape=jax.ShapeDtypeStruct((query_rows,...]
where the time goes in v3:
time: 31 us; the launch traced here: 30.8 us
  Pallas kernels  28.7 us (93%)
  local copies, waits for them, and re-layouts  1.45 us (5%)
  between operations  0.64 us (2%)
    pallas_call x1, Pallas kernels, shards(): pl.pallas_call(search_kernel, out_shape=jax.ShapeDtypeStruct((query_rows,...  28.7 us
    slice x1, local copies, waits for them, and re-layouts, shards(): return (out[:, :TOPK], out[:, TOPK:])  1.45 us

profile of v3, /device:TPU:0, one launch (start us, length us, event | category | flops | bytes accessed | tf_op | source)
XLA Modules:
  0.0 30.8 jit_solution(10628684168825056669)
XLA Ops:
  0.6 28.7 %search.1 = f32[16,64]{1,0:T(8,128)} custom-call(bf16[16,2048]{1,0:T(8,128)(2,1)} %q_hbm.1, s32[16,16]{1,0:T(8,128)} %pd_hbm.1, s32[16,16]{1,0:T(8,128)} %pl_hbm.1, s32[16,32]{1,0:T(8,128)} %sd_hbm.1, s32[16,32]{1,0:T(8,128)} %sl_hbm.1, s32[16,32]{1,0:T(8,128)} %sr_hbm.1, s32[16]{0:T(128)} %len_ref.1, bf16[16,256,2048]{2,1,0:T(8,128)(2,1)} %docs_hbm.1), custom_call_target="tpu_custom_call" | custom-call | tf_op jit(solution)/shard_map/search/pallas_call | solution.py:373
  29.3 1.4 %fusion = (f32[16,32]{1,0:T(8,128)}, f32[16,32]{1,0:T(8,128)}) fusion(f32[16,64]{1,0:T(8,128)} %search.1), kind=kLoop, calls=%fused_computation | loop fusion | bytes 8192 | tf_op jit(solution)/shard_map/slice | solution.py:415

commit v4 on v3

--- a/solution.py
+++ b/solution.py
@@ -67,12 +67,12 @@
 
 
 def search_kernel(
-    q_hbm, pd_hbm, pl_hbm, sd_hbm, sl_hbm, sr_hbm, len_ref, docs_hbm, out_ref, *scratch,
+    q_hbm, pd_hbm, pl_hbm, sd_hbm, sl_hbm, sr_hbm, len_hbm, docs_hbm, out_ref, *scratch,
 ):
     cuts = column_cuts(q_hbm.shape[1])
     chunks = len(cuts) - 1
     gathered = scratch[:chunks]
-    (queries, pd, plist, sd, sl, sr, pre_docs, top_docs, unit, spots, chosen, result,
+    (queries, len_ref, pd, plist, sd, sl, sr, pre_docs, top_docs, unit, spots, chosen, result,
      ret, got, acc, part_ret, part_got, load_sem, docs_sem, send_sem, line_recv, plane_recv, core_recv,
      top_sem, part_sem) = scratch[chunks:]
     gx, gy = lax.axis_index("gx"), lax.axis_index("gy")
@@ -126,6 +126,8 @@
         copy.start()
     whole = pltpu.make_async_copy(q_hbm, queries, load_sem.at[5])
     whole.start()
+    counts = pltpu.make_async_copy(len_hbm, len_ref, load_sem.at[6])
+    counts.start()
     pre_copies = [
         pltpu.make_async_copy(docs_hbm.at[:, :, columns(k)], pre_docs.at[k], docs_sem.at[k]) for k in range(head)
     ]
@@ -293,6 +295,7 @@
     for c in range(chunks):
         spread(c)
     share(0)
+    counts.wait()
     for copy in pre_copies:
         copy.wait()
     for t in halves[0]:
@@ -368,12 +371,12 @@
     packed = query_rows * TOPK // LANES
     extra = 2 * probes + 3 * shorts
     vmem = pl.BlockSpec(memory_space=pltpu.VMEM)
-    hbm = pl.BlockSpec(memory_space=pl.ANY)
+    hbm = pl.BlockSpec(memory_space=pltpu.HBM)
     dma = pltpu.SemaphoreType.DMA
     out = pl.pallas_call(
         search_kernel,
         out_shape=jax.ShapeDtypeStruct((query_rows, TOPK + shorts), jnp.float32),
-        in_specs=[hbm] * 6 + [pl.BlockSpec(memory_space=pltpu.SMEM), hbm],
+        in_specs=[hbm] * 8,
         out_specs=vmem,
         scratch_shapes=[
             pltpu.VMEM(
@@ -382,6 +385,7 @@
             for c in range(chunks)
         ] + [
             pltpu.VMEM((query_rows, full), jnp.bfloat16),
+            pltpu.SMEM((lists,), jnp.int32),
             pltpu.VMEM((query_rows, probes), jnp.int32),
             pltpu.VMEM((query_rows, probes), jnp.int32),
             pltpu.VMEM((query_rows, shorts), jnp.int32),

time: 31 us -> 30.3 us (0.977)
  Pallas kernels: 28.7 us -> 28 us
    pallas_call x1, Pallas kernels: 28.7 us -> 28 us  [shards(): pl.pallas_call(search_kernel, out_shape=jax.ShapeDtypeStruct((query_rows,...]
where the time goes in v4:
time: 30.3 us; the launch traced here: 30.1 us
  Pallas kernels  28 us (92%)
  local copies, waits for them, and re-layouts  1.45 us (5%)
  between operations  0.64 us (2%)
    pallas_call x1, Pallas kernels, shards(): pl.pallas_call(search_kernel, out_shape=jax.ShapeDtypeStruct((query_rows,...  28 us
    slice x1, local copies, waits for them, and re-layouts, shards(): return (out[:, :TOPK], out[:, TOPK:])  1.45 us

profile of v4, /device:TPU:0, one launch (start us, length us, event | category | flops | bytes accessed | tf_op | source)
XLA Modules:
  0.0 30.1 jit_solution(3975453557935673097)
XLA Ops:
  0.6 28.0 %search.1 = f32[16,64]{1,0:T(8,128)} custom-call(bf16[16,2048]{1,0:T(8,128)(2,1)} %q_hbm.1, s32[16,16]{1,0:T(8,128)} %pd_hbm.1, s32[16,16]{1,0:T(8,128)} %pl_hbm.1, s32[16,32]{1,0:T(8,128)} %sd_hbm.1, s32[16,32]{1,0:T(8,128)} %sl_hbm.1, s32[16,32]{1,0:T(8,128)} %sr_hbm.1, s32[16]{0:T(128)} %len_hbm.1, bf16[16,256,2048]{2,1,0:T(8,128)(2,1)} %docs_hbm.1), custom_call_target="tpu_custom_call" | custom-call | tf_op jit(solution)/shard_map/search/pallas_call | solution.py:376
  28.7 1.4 %fusion = (f32[16,32]{1,0:T(8,128)}, f32[16,32]{1,0:T(8,128)}) fusion(f32[16,64]{1,0:T(8,128)} %search.1), kind=kLoop, calls=%fused_computation | loop fusion | bytes 8192 | tf_op jit(solution)/shard_map/slice | solution.py:419
